TPU v7x, 32 devices: a whole 2x2x4 slice. The times are simulated.
32 devices in a mesh: dp: 4 (over z), mp: 8 (over y, x, core).
Axes of the slice: x: 2, y: 2, z: 4, core: 2. Of those that a mesh axis runs over, the one named last changes fastest.
Arguments:
- grad_parts: bfloat16 [4, 8, 2, 18432, 128], P('dp', 'mp'), may hold values from -45 to 45
- master: float32 [8, 2, 18432, 128], P('mp', None, 'dp'), may hold values from -15 to 15
- momenta: float32 [3, 8, 2, 18432, 128], P(None, 'mp', None, 'dp'), may hold values from -45 to 45
- second: float32 [3, 8, 2, 18432, 128], P(None, 'mp', None, 'dp'), may hold values from 0.00025 to 330
- step_count: int32 [1], replicated, may hold values from 1 to 99999
- mlp_first: float32 [8, 4], replicated, may hold values from -2 to 2
- mlp_bias: float32 [4], replicated, may hold values from -3 to 3
- mlp_second: float32 [4, 2], replicated, may hold values from -3 to 3
- tensor_weight: float32 [10], replicated, may hold values from -2 to 2
Outputs:
- new_params: bfloat16 [8, 2, 18432, 128], P('mp')
- new_master: float32 [8, 2, 18432, 128], P('mp', None, 'dp')
- new_momenta: float32 [3, 8, 2, 18432, 128], P(None, 'mp', None, 'dp')
- new_second: float32 [3, 8, 2, 18432, 128], P(None, 'mp', None, 'dp')
- update: float32 [8, 2, 18432, 128], P('mp', None, 'dp')
All inputs are finite; a program needn't handle non-finite values.
Results may differ from a plain program's by a relative error of at most 0.019.
Values may be sent and summed in bfloat16 or wider, within the bound.
A program may use at most 192 MiB of HBM per device.

v0:
```python
import jax
import jax.numpy as jnp
from jax import lax
from jax.sharding import PartitionSpec as P

D = 4608
HQ = 4096
RATES = (0.9, 0.99, 0.999)


def advance(gradient, momenta, second):
    moments = jnp.stack(
        [rate * momenta[i] + (1.0 - rate) * gradient for i, rate in enumerate(RATES)]
    )
    squares = jnp.stack(
        [rate * second[i] + (1.0 - rate) * gradient * gradient for i, rate in enumerate(RATES)]
    )
    return (moments, squares)


def features_of(master, gradient, moments, squares):
    listing = [master, gradient, moments[0], moments[1], moments[2]]
    for slot_id in range(3):
        listing.append(moments[slot_id] / jnp.sqrt(squares[slot_id]))
    return listing


def perceptron(normed, boost, mlp_first, mlp_bias, mlp_second):
    direction = jnp.zeros_like(normed[0])
    magnitude = jnp.zeros_like(normed[0])
    for unit_id in range(mlp_first.shape[1]):
        active = mlp_first[0, unit_id] * normed[0]
        for feat_id in range(1, len(normed)):
            active = active + mlp_first[feat_id, unit_id] * normed[feat_id]
        active = jax.nn.relu(active + mlp_bias[unit_id])
        direction = direction + mlp_second[unit_id, 0] * active
        magnitude = magnitude + mlp_second[unit_id, 1] * active
    return direction * jnp.exp(0.5 * jnp.tanh(magnitude)) * boost


def tensor_boost(norms, step_count, tensor_weight):
    count = tensor_weight.shape[0] - 2
    step_value = step_count[0].astype(jnp.float32)
    first_phase = jnp.log1p(step_value) / 11.5
    second_phase = step_value / 100000.0
    logits = jnp.sum(tensor_weight[:count, None] * jnp.log(norms), axis=0)
    logits = logits + tensor_weight[count] * first_phase + tensor_weight[count + 1] * second_phase
    return jnp.exp(jnp.tanh(logits))


def square_sums(listing):
    return jnp.stack([jnp.sum(feature * feature, axis=(0, 2, 3)) for feature in listing])


def local(
    grad_parts, master, momenta, second, step_count, mlp_first, mlp_bias, mlp_second, tensor_weight
):
    gradient = lax.psum_scatter(grad_parts, "dp", scatter_dimension=3, tiled=True).astype(
        jnp.float32
    )[0]
    new_momenta, new_second = advance(gradient, momenta, second)
    early_local = square_sums([master, gradient])
    listing = features_of(master, gradient, new_momenta, new_second)
    late_local = square_sums(listing[2:])
    totals = lax.psum(jnp.concatenate([early_local, late_local], axis=0), ("dp", "mp"))
    norms = jnp.sqrt(totals / float(D * HQ) + 1e-06)
    boost = tensor_boost(norms, step_count, tensor_weight)[None, :, None, None]
    normed = [listing[i] / norms[i][None, :, None, None] for i in range(len(listing))]
    update = perceptron(normed, boost, mlp_first, mlp_bias, mlp_second)
    new_master = master - 0.05 * update
    new_params = lax.all_gather(new_master.astype(jnp.bfloat16), "dp", axis=2, tiled=True)
    return (new_params, new_master, new_momenta, new_second, update)


def solution(mesh):
    placed = (
        P("dp", "mp", None, None, None),
        P("mp", None, "dp", None),
        P(None, "mp", None, "dp", None),
        P(None, "mp", None, "dp", None),
        P(),
        P(),
        P(),
        P(),
        P(),
    )
    return jax.shard_map(
        local,
        mesh=mesh,
        in_specs=placed,
        out_specs=(
            P("mp", None, None, None),
            P("mp", None, "dp", None),
            P(None, "mp", None, "dp", None),
            P(None, "mp", None, "dp", None),
            P("mp", None, "dp", None),
        ),
        check_vma=False,
    )
```

profile of v0, /device:TPU:0, one launch (start us, length us, event | category | flops | bytes accessed | tf_op | source)
XLA Modules:
  0.0 466.4 jit_solution(5703901997524263589)
XLA Ops:
  7.2 0.0 reduce-scatter.2.cloned.1.call-start
  7.2 0.7 reduce-scatter.2.cloned.1.call-update
  7.9 0.0 copy-start.4
  7.9 0.0 copy-start.3
  7.9 0.0 copy-start.2
  7.9 0.0 copy-start.1
  7.9 0.0 all-gather.2.cloned.1.call-start
  8.7 3.0 multiply_reduce_fusion.6
  11.7 0.1 copy.22
  11.8 0.0 copy-done.4
  11.8 0.6 fusion.33
  13.1 0.0 copy-done.3
  13.1 0.6 fusion.32
  13.7 0.0 copy-done.2
  13.7 0.7 fusion.31
  14.4 0.0 copy-done.1
  14.4 0.7 fusion.30
  15.1 0.7 fusion.29
  15.9 158.4 %reduce-scatter.2.cloned.1.call-done = bf16[1,1,2,4608,128]{4,3,2,1,0:T(8,128)(2,1)} async-done(((bf16[1,1,2,18432,128]{4,3,2,1,0:T(8,128)(2,1)}), bf16[1,1,2,4608,128]{4,3,2,1,0:T(8,128)(2,1)}) %reduce-scatter.2.cloned.1.call-update) | async-done | bytes 2359312 | tf_op jit(solution)/shard_map/reduce_scatter | solution.py:58
  174.3 0.0 copy-start
  174.3 14.4 %multiply_reduce_fusion = (f32[2]{0:T(128)S(1)}, f32[2]{0:T(128)S(1)}, f32[2]{0:T(128)S(1)}, f32[2]{0:T(128)S(1)}, f32[2]{0:T(128)S(1)}, /*index=5*/f32[2]{0:T(128)S(1)}, f32[2]{0:T(128)S(1)}) fusion(bf16[1,1,2,4608,128]{4,3,2,1,0:T(8,128)(2,1)} %reduce-scatter.2.cloned.1.call-done, f32[3,1,2,4608,128]{4,3,2,1,0:T(8,128)} %param.12, ...), kind=kLoop, calls=%fused_computation.38 | loop fusion | flops 42467320 | bytes 30670904 | tf_op jit(solution)/shard_map/reduce_sum | solution.py:52
  188.7 0.1 copy.27
  188.8 0.1 copy.29
  188.9 0.1 copy.28
  189.0 0.1 copy.24
  189.1 0.1 copy.25
  189.2 0.1 copy.26
  189.2 0.1 copy.23
  189.3 0.1 concatenate.3
  190.1 41.2 %psum.7 = f32[8,2]{0,1:T(2,128)S(1)} all-reduce(f32[8,2]{0,1:T(2,128)S(1)} %concatenate.3), channel_id=1, replica_groups=mesh['dp'=4,'mp'=8] {'dp','mp'}, use_global_device_ids=true, to_apply=%region_9.0 | all-reduce | flops 16 | bytes 128 | tf_op jit(solution)/shard_map/psum | solution.py:65
  231.3 0.1 fusion.27
  231.4 0.3 slice_reduce_fusion.7
  231.7 0.0 copy-done
  231.7 52.0 %fusion.28 = (bf16[1,2,4608,128]{3,2,1,0:T(8,128)(2,1)}, f32[1,2,4608,128]{3,2,1,0:T(8,128)}, f32[1,2,4608,128]{3,2,1,0:T(8,128)}) fusion(f32[1,2,4608,128]{3,2,1,0:T(8,128)} %param.10, f32[2]{0:T(128)S(1)} %tanh_exponential_fusion, f32[]{:T(128)} %bitcast.58, f32[]{:T(128)} %bitcast.57, f32[]{:T(128)} %bitcast.56, f32[]{:T(128)} %bitcast.55, f32[]{:T(128)} %bitcast.54, ...), kind=kLoop, calls=%fused_computation.64 | loop fusion | flops 139198464 | bytes 47186168 | tf_op jit(solution)/shard_map/convert_element_type | solution.py:71
  283.7 0.0 all-gather.2.cloned.1.call-update
  283.7 20.3 %fusion.24 = (f32[1,1,2,4608,128]{4,3,2,1,0:T(8,128)}, f32[1,1,2,4608,128]{4,3,2,1,0:T(8,128)}, f32[1,1,2,4608,128]{4,3,2,1,0:T(8,128)}, f32[1,1,2,4608,128]{4,3...) fusion(bf16[1,1,2,4608,128]{4,3,2,1,0:T(8,128)(2,1)S(1)} %copy-done, ...), kind=kLoop, calls=%fused_computation.33 | loop fusion | flops 22413312 | bytes 58982400 | tf_op jit(solution)/shard_map/add | solution.py:16
  304.1 18.9 %pad_maximum_fusion = (f32[3,1,2,4608,128]{4,3,2,1,0:T(8,128)}, f32[3,1,2,4608,128]{4,3,2,1,0:T(8,128)}) fusion(f32[1,1,2,4608,128]{4,3,2,1,0:T(8,128)} %get-tuple-element.29, f32[1,1,2,4608,128]{4,3,2,1,0:T(8,128)} %get-tuple-element.30, f32[1,1,2,4608,128]{4,3,2,1,0:T(8,128)} %get-tuple-element.31, f32[1,1,2,4608,128]{4,3,2,1,0:T(8,128)} %get-tuple-element.25, ...), kind=kLoop, calls=%fused_computation | loop fusion | flops 14155776 | bytes 56623104 | tf_op jit(solution)/shard_map/stack | solution.py:12
  323.0 127.5 %all-gather.2.cloned.1.call-done = bf16[1,2,18432,128]{3,2,1,0:T(8,128)(2,1)} async-done(((bf16[1,2,4608,128]{3,2,1,0:T(8,128)(2,1)}), bf16[1,2,18432,128]{3,2,1,0:T(8,128)(2,1)}) %all-gather.2.cloned.1.call-update) | async-done | bytes 9437200 | tf_op jit(solution)/shard_map/all_gather | solution.py:71
  450.4 9.1 %copy.32 = bf16[1,2,18432,128]{3,2,1,0:T(8,128)(2,1)} copy(bf16[1,2,18432,128]{3,2,1,0:T(8,128)(2,1)} %all-gather.2.cloned.1.call-done) | data formatting | bytes 18874368
  (2 shorter events, 0.0 us)
Async XLA Ops:
  7.2 167.1 %reduce-scatter.2.cloned.1.call-start = ((), (), s32[]{:S(2)}) async-start(), calls=%async_computation.1 | async-start | bytes 11796480 | tf_op jit(solution)/shard_map/reduce_scatter | solution.py:58
  7.9 3.9 copy-start.4
  7.9 5.1 %copy-start.3 = (f32[4]{0:T(128)S(1)}, f32[4]{0:T(128)}, u32[]{:S(2)}) copy-start(f32[4]{0:T(128)} %param.15) | copy-start | bytes 52
  7.9 5.8 %copy-start.2 = (f32[4,2]{0,1:T(2,128)S(1)}, f32[4,2]{0,1:T(2,128)}, u32[]{:S(2)}) copy-start(f32[4,2]{0,1:T(2,128)} %param.16) | copy-start | bytes 100
  7.9 6.5 %copy-start.1 = (f32[8,4]{0,1:T(4,128)S(1)}, f32[8,4]{0,1:T(4,128)}, u32[]{:S(2)}) copy-start(f32[8,4]{0,1:T(4,128)} %param.14) | copy-start | bytes 388
  7.9 442.5 %all-gather.2.cloned.1.call-start = ((), (), s32[]{:S(2)}) async-start(), calls=%async_computation.2 | async-start | bytes 11796480 | tf_op jit(solution)/shard_map/all_gather | solution.py:71
  174.3 57.4 %copy-start = (bf16[1,1,2,4608,128]{4,3,2,1,0:T(8,128)(2,1)S(1)}, bf16[1,1,2,4608,128]{4,3,2,1,0:T(8,128)(2,1)}, u32[]{:S(2)}) copy-start(bf16[1,1,2,4608,128]{4,3,2,1,0:T(8,128)(2,1)} %reduce-scatter.2.cloned.1.call-done) | copy-start | bytes 7077892
Sparse Core Ops, SparseCore 0:
  10.3 163.9 reduce-scatter.1
  283.9 166.5 all-gather.1
where the time goes:
time: 467 us; the launch traced here: 466 us
  waiting for transfers between devices  287 us (61%)
  other arithmetic  109 us (23%)
  blocking collectives  41.2 us (9%)
  between operations  16.1 us (3%)
  local copies, waits for them, and re-layouts  13.6 us (3%)
    reduce_scatter x1, waiting for transfers between devices, local(): lax.psum_scatter(grad_parts, 'dp', scatter_dimension=3, tiled=True)  158 us
    all_gather x1, waiting for transfers between devices, local(): lax.all_gather(new_master.astype(jnp.bfloat16), 'dp', axis=2, tiled=True)  127 us
    convert_element_type x1, other arithmetic, local(): new_master.astype(jnp.bfloat16)  52 us
    psum x1, blocking collectives, local(): lax.psum(jnp.concatenate([early_local, late_local], axis=0), ('dp', 'mp'))  41.2 us
    add x1, other arithmetic, advance(): rate * second[i] + (1.0 - rate) * gradient * gradient  20.3 us
    another operation x1, other arithmetic, advance(): jnp.stack([rate * momenta[i] + (1.0 - rate) * gradient for i, rate in enu...  18.9 us
    reduce_sum x2, other arithmetic, square_sums(): jnp.sum(feature * feature, axis=(0, 2, 3))  17.4 us
  transfers between devices with their start and end apart: 2, of which 2 were waited for; matrix products, arithmetic and copies ran while one was open for 10% of the time, Pallas kernels for 0%

commit v1 on v0

--- a/solution.py
+++ b/solution.py
@@ -68,7 +68,13 @@
     normed = [listing[i] / norms[i][None, :, None, None] for i in range(len(listing))]
     update = perceptron(normed, boost, mlp_first, mlp_bias, mlp_second)
     new_master = master - 0.05 * update
-    new_params = lax.all_gather(new_master.astype(jnp.bfloat16), "dp", axis=2, tiled=True)
+    obj = new_master.astype(jnp.bfloat16)
+    new_params = jnp.concatenate(
+        lax.all_to_all(
+            jnp.stack([obj for _ in range(lax.axis_size("dp"))]), "dp", split_axis=0, concat_axis=0
+        ),
+        axis=2,
+    )
     return (new_params, new_master, new_momenta, new_second, update)
 
 

time: 467 us -> 515 us (1.10)
  waiting for transfers between devices: 287 us -> 326 us
  starting transfers between devices: 0.08 us -> 6.03 us
    all_to_all x0 -> x1, waiting for transfers between devices: none -> 167 us  [local(): lax.all_to_all(jnp.stack([obj for _ in range(lax.axis_size('dp'))]), 'dp'...]
    all_gather x1 -> x0, waiting for transfers between devices: 127 us -> none  [local(): lax.all_gather(new_master.astype(jnp.bfloat16), 'dp', axis=2, tiled=True)]
    unnamed x11 -> x10, local copies, waits for them, and re-layouts: 9.14 us -> 0.02 us
    all_to_all x0 -> x1, local copies, waits for them, and re-layouts: none -> 8.1 us  [local(): lax.all_to_all(jnp.stack([obj for _ in range(lax.axis_size('dp'))]), 'dp'...]
    all_to_all x0 -> x1, starting transfers between devices: none -> 5.99 us  [local(): lax.all_to_all(jnp.stack([obj for _ in range(lax.axis_size('dp'))]), 'dp'...]
  transfers between devices with their start and end apart: 2 -> 2, of which waited for: 2 -> 2; matrix products, arithmetic and copies ran while one was open for 10% -> 9% of each run, Pallas kernels for 0% -> 0%
where the time goes in v1:
time: 515 us; the launch traced here: 514 us
  waiting for transfers between devices  326 us (63%)
  other arithmetic  108 us (21%)
  blocking collectives  41.2 us (8%)
  local copies, waits for them, and re-layouts  17.6 us (3%)
  between operations  16.1 us (3%)
  starting transfers between devices  6.03 us (1%)
    all_to_all x1, waiting for transfers between devices, local(): lax.all_to_all(jnp.stack([obj for _ in range(lax.axis_size('dp'))]), 'dp'...  167 us
    reduce_scatter x1, waiting for transfers between devices, local(): lax.psum_scatter(grad_parts, 'dp', scatter_dimension=3, tiled=True)  158 us
    convert_element_type x1, other arithmetic, local(): obj = new_master.astype(jnp.bfloat16)  51.7 us
    psum x1, blocking collectives, local(): lax.psum(jnp.concatenate([early_local, late_local], axis=0), ('dp', 'mp'))  41.2 us
    add x1, other arithmetic, advance(): rate * second[i] + (1.0 - rate) * gradient * gradient  19.7 us
    another operation x1, other arithmetic, advance(): jnp.stack([rate * momenta[i] + (1.0 - rate) * gradient for i, rate in enu...  18.6 us
    reduce_sum x2, other arithmetic, square_sums(): jnp.sum(feature * feature, axis=(0, 2, 3))  17.4 us
  transfers between devices with their start and end apart: 2, of which 2 were waited for; matrix products, arithmetic and copies ran while one was open for 9% of the time, Pallas kernels for 0%

profile of v1, /device:TPU:0, one launch (start us, length us, event | category | flops | bytes accessed | tf_op | source)
XLA Modules:
  0.0 514.1 jit_solution(8666093548195073739)
XLA Ops:
  7.2 0.0 reduce-scatter.2.cloned.1.call-start
  7.2 0.7 reduce-scatter.2.cloned.1.call-update
  7.9 0.0 copy-start.4
  7.9 0.0 copy-start.3
  7.9 0.0 copy-start.2
  7.9 0.0 copy-start.1
  8.7 3.0 multiply_reduce_fusion.6
  11.7 0.1 copy.22
  11.8 0.0 copy-done.4
  11.8 0.6 fusion.32
  13.0 0.0 copy-done.3
  13.1 0.6 fusion.31
  13.7 0.0 copy-done.2
  13.7 0.7 fusion.30
  14.4 0.0 copy-done.1
  14.4 0.7 fusion.29
  15.1 0.7 fusion.28
  15.8 158.4 %reduce-scatter.2.cloned.1.call-done = bf16[1,1,2,4608,128]{4,3,2,1,0:T(8,128)(2,1)} async-done(((bf16[1,1,2,18432,128]{4,3,2,1,0:T(8,128)(2,1)}), bf16[1,1,2,4608,128]{4,3,2,1,0:T(8,128)(2,1)}) %reduce-scatter.2.cloned.1.call-update) | async-done | bytes 2359312 | tf_op jit(solution)/shard_map/reduce_scatter | solution.py:58
  174.3 0.0 copy-start
  174.3 14.4 %multiply_reduce_fusion = (f32[2]{0:T(128)S(1)}, f32[2]{0:T(128)S(1)}, f32[2]{0:T(128)S(1)}, f32[2]{0:T(128)S(1)}, f32[2]{0:T(128)S(1)}, /*index=5*/f32[2]{0:T(128)S(1)}, f32[2]{0:T(128)S(1)}) fusion(bf16[1,1,2,4608,128]{4,3,2,1,0:T(8,128)(2,1)} %reduce-scatter.2.cloned.1.call-done, f32[3,1,2,4608,128]{4,3,2,1,0:T(8,128)} %param.12, ...), kind=kLoop, calls=%fused_computation.38 | loop fusion | flops 42467320 | bytes 30670904 | tf_op jit(solution)/shard_map/reduce_sum | solution.py:52
  188.7 0.1 copy.27
  188.8 0.1 copy.29
  188.9 0.1 copy.28
  189.0 0.1 copy.24
  189.1 0.1 copy.25
  189.2 0.1 copy.26
  189.2 0.1 copy.23
  189.3 0.1 concatenate.3
  190.1 41.2 %psum.7 = f32[8,2]{0,1:T(2,128)S(1)} all-reduce(f32[8,2]{0,1:T(2,128)S(1)} %concatenate.3), channel_id=1, replica_groups=mesh['dp'=4,'mp'=8] {'dp','mp'}, use_global_device_ids=true, to_apply=%region_9.0 | all-reduce | flops 16 | bytes 128 | tf_op jit(solution)/shard_map/psum | solution.py:65
  231.3 0.1 fusion.27
  231.4 0.3 slice_reduce_fusion.7
  231.7 0.0 copy-done
  231.7 51.7 %convert_bitcast_fusion.1 = (bf16[2,4608,128]{2,1,0:T(8,128)(2,1)S(1)}, f32[1,2,4608,128]{3,2,1,0:T(8,128)}, f32[1,2,4608,128]{3,2,1,0:T(8,128)}) fusion(f32[1,2,4608,128]{3,2,1,0:T(8,128)} %param.10, f32[2]{0:T(128)S(1)} %tanh_exponential_fusion, f32[]{:T(128)} %bitcast.58, f32[]{:T(128)} %bitcast.57, f32[]{:T(128)} %bitcast.56, f32[]{:T(128)} %bitcast.55, ...), kind=kLoop, calls=%fused_computation.51 | loop fusion | flops 139198464 | bytes 47186168 | tf_op jit(solution)/shard_map/convert_element_type | solution.py:71
  283.4 5.0 stack.51
  288.4 6.0 %all-to-all-start = ((bf16[4,1,2,4608,128]{4,3,2,1,0:T(8,128)(2,1)}), bf16[4,1,2,4608,128]{4,3,2,1,0:T(8,128)(2,1)}, u32[]{:S(2)}, u32[]{:S(2)}) async-start(bf16[4,1,2,4608,128]{4,3,2,1,0:T(8,128)(2,1)} %stack.51), calls=%async_computation.1 | async-start | bytes 18874368 | tf_op jit(solution)/shard_map/all_to_all | solution.py:73
  294.4 19.7 %fusion.24 = (f32[1,1,2,4608,128]{4,3,2,1,0:T(8,128)}, f32[1,1,2,4608,128]{4,3,2,1,0:T(8,128)}, f32[1,1,2,4608,128]{4,3,2,1,0:T(8,128)}, f32[1,1,2,4608,128]{4,3...) fusion(bf16[1,1,2,4608,128]{4,3,2,1,0:T(8,128)(2,1)S(1)} %copy-done, ...), kind=kLoop, calls=%fused_computation.33 | loop fusion | flops 22413312 | bytes 58982400 | tf_op jit(solution)/shard_map/add | solution.py:16
  314.1 18.6 %pad_maximum_fusion = (f32[3,1,2,4608,128]{4,3,2,1,0:T(8,128)}, f32[3,1,2,4608,128]{4,3,2,1,0:T(8,128)}) fusion(f32[1,1,2,4608,128]{4,3,2,1,0:T(8,128)} %get-tuple-element.29, f32[1,1,2,4608,128]{4,3,2,1,0:T(8,128)} %get-tuple-element.30, f32[1,1,2,4608,128]{4,3,2,1,0:T(8,128)} %get-tuple-element.31, f32[1,1,2,4608,128]{4,3,2,1,0:T(8,128)} %get-tuple-element.25, ...), kind=kLoop, calls=%fused_computation | loop fusion | flops 14155776 | bytes 56623104 | tf_op jit(solution)/shard_map/stack | solution.py:12
  332.6 166.6 %all-to-all-done = bf16[4,1,2,4608,128]{4,3,2,1,0:T(8,128)(2,1)} async-done(((bf16[4,1,2,4608,128]{4,3,2,1,0:T(8,128)(2,1)}), bf16[4,1,2,4608,128]{4,3,2,1,0:T(8,128)(2,1)}, u32[]{:S(2)}, u32[]{:S(2)}) %all-to-all-start) | async-done | bytes 9437216 | tf_op jit(solution)/shard_map/all_to_all | solution.py:73
  499.2 8.1 %copy.30 = bf16[4,1,2,4608,128]{4,3,0,2,1:T(8,128)(2,1)} copy(bf16[4,1,2,4608,128]{4,3,2,1,0:T(8,128)(2,1)} %all-to-all-done) | data formatting | bytes 18874368 | tf_op jit(solution)/shard_map/all_to_all | solution.py:73
  (2 shorter events, 0.0 us)
Async XLA Ops:
  7.2 167.1 %reduce-scatter.2.cloned.1.call-start = ((), (), s32[]{:S(2)}) async-start(), calls=%async_computation.2 | async-start | bytes 11796480 | tf_op jit(solution)/shard_map/reduce_scatter | solution.py:58
  7.9 3.9 copy-start.4
  7.9 5.1 copy-start.3
  7.9 5.8 %copy-start.2 = (f32[4,2]{0,1:T(2,128)S(1)}, f32[4,2]{0,1:T(2,128)}, u32[]{:S(2)}) copy-start(f32[4,2]{0,1:T(2,128)} %param.16) | copy-start | bytes 100
  7.9 6.5 %copy-start.1 = (f32[8,4]{0,1:T(4,128)S(1)}, f32[8,4]{0,1:T(4,128)}, u32[]{:S(2)}) copy-start(f32[8,4]{0,1:T(4,128)} %param.14) | copy-start | bytes 388
  174.3 57.4 %copy-start = (bf16[1,1,2,4608,128]{4,3,2,1,0:T(8,128)(2,1)S(1)}, bf16[1,1,2,4608,128]{4,3,2,1,0:T(8,128)(2,1)}, u32[]{:S(2)}) copy-start(bf16[1,1,2,4608,128]{4,3,2,1,0:T(8,128)(2,1)} %reduce-scatter.2.cloned.1.call-done) | copy-start | bytes 7077892
  288.4 210.8 %all-to-all-start = ((bf16[4,1,2,4608,128]{4,3,2,1,0:T(8,128)(2,1)}), bf16[4,1,2,4608,128]{4,3,2,1,0:T(8,128)(2,1)}, u32[]{:S(2)}, u32[]{:S(2)}) async-start(bf16[4,1,2,4608,128]{4,3,2,1,0:T(8,128)(2,1)} %stack.51), calls=%async_computation.1 | async-start | bytes 18874368 | tf_op jit(solution)/shard_map/all_to_all | solution.py:73
Sparse Core Ops, SparseCore 0:
  10.3 163.9 reduce-scatter.1
